TPU v7x, 32 devices: a whole 2x2x4 slice. The times are simulated.
32 devices in a mesh: blk: 2 (over y), uly: 4 (over x, core), dp: 4 (over z).
Axes of the slice: x: 2, y: 2, z: 4, core: 2. Of those that a mesh axis runs over, the one named last changes fastest.
Arguments:
- tokens: bfloat16 [1024, 4096], P(('uly', 'dp')), may hold values from -6 to 6
- expert_ids: int32 [1024, 8], P(('uly', 'dp')), may hold values from 0 to 15, all different within a row; in each aligned block of 64 rows (0 to 63, 64 to 127, ...) at most 40 rows name the same one
- route_weight: float32 [1024, 8], P(('uly', 'dp')), may hold values from 0.05 to 0.5
- w_gate: bfloat16 [16, 4096, 1024], P(('uly', 'dp'), None, 'blk'), may hold values from -0.09375 to 0.09375
- w_up: bfloat16 [16, 4096, 1024], P(('uly', 'dp'), None, 'blk'), may hold values from -0.09375 to 0.09375
- w_down: bfloat16 [16, 1024, 4096], P(('uly', 'dp'), 'blk'), may hold values from -0.1875 to 0.1875
Outputs:
- mixed: bfloat16 [1024, 4096], P(('uly', 'dp'), 'blk')
Inputs may be any that keep to these rules, and one draw needn't show every extreme that they name: `expert_ids`: each row names 8 different experts. In each aligned block of 64 rows (the rows of one device) no expert is named by more than 40 rows, and in some block one expert is named by exactly 40 rows.
All inputs are finite; a program needn't handle non-finite values.
Results may differ from a plain program's by a relative error of at most 0.015.
Values may be sent and summed in bfloat16 or wider, within the bound.
A program may use at most 64 MiB of HBM per device.

v0:
```python
import jax
import jax.numpy as jnp
from jax import lax
from jax.experimental import pallas as pl
from jax.experimental.pallas import tpu as pltpu
from jax.sharding import PartitionSpec as P


def routing_tables(expert_ids, route_weight, groups, local_count, capacity):
    tokens_here, picks_count = expert_ids.shape
    experts = groups * local_count
    labels = lax.broadcasted_iota(jnp.int32, (1, 1, experts), 2)
    onehot = (expert_ids[:, :, None] == labels).astype(jnp.int32)
    chosen = jnp.sum(onehot, axis=1)
    before = jnp.cumsum(chosen, axis=0) - chosen
    slot_of = jnp.sum(onehot * before[:, None, :], axis=2)
    places = lax.broadcasted_iota(jnp.int32, (1, 1, capacity), 2)
    slot_hot = (slot_of[:, :, None] == places).astype(jnp.float32)
    expert_hot = onehot.astype(jnp.float32).reshape(tokens_here, picks_count, groups, local_count)
    placing = jnp.einsum("tkgl,tkc->gclt", expert_hot, slot_hot)
    placing = placing.reshape(groups * capacity * local_count, tokens_here)
    mixing = jnp.einsum("tkgl,tkc,tk->tgcl", expert_hot, slot_hot, route_weight)
    mixing = mixing.reshape(tokens_here, groups * capacity * local_count)
    return (placing.astype(jnp.bfloat16), mixing)


def local_slots(tokens, expert_ids, route_weight, w_gate, w_up, w_down):
    ulysses_size = lax.axis_size("uly")
    data_size = lax.axis_size("dp")
    cycle_size = lax.axis_size("blk")
    tokens_here, model_width = tokens.shape
    local_count = w_gate.shape[0]
    hidden_cut = w_gate.shape[2]
    groups = ulysses_size * data_size
    experts = groups * local_count
    picks_count = expert_ids.shape[1]
    capacity = min(tokens_here, max(2, 5 * tokens_here * picks_count // (4 * experts)))
    placing, mixing = routing_tables(expert_ids, route_weight, groups, local_count, capacity)
    slice_width = model_width // cycle_size
    rows_total = groups * capacity
    cycle_index = lax.axis_index("blk")
    own_part = lax.dynamic_slice_in_dim(tokens, cycle_index * slice_width, slice_width, 1)
    outgoing = jnp.dot(placing, own_part, preferred_element_type=jnp.float32).astype(jnp.bfloat16)
    outgoing = outgoing.reshape(ulysses_size, data_size, capacity, local_count, slice_width)
    arrived = lax.all_to_all(
        lax.all_to_all(outgoing, "uly", split_axis=0, concat_axis=0, tiled=True),
        "dp",
        split_axis=1,
        concat_axis=1,
        tiled=True,
    )
    arrived = arrived.reshape(rows_total, local_count, slice_width)
    portion = lax.all_gather(arrived, "blk", axis=2, tiled=True)
    gate_more = jnp.einsum("rlw,lwf->rlf", portion, w_gate, preferred_element_type=jnp.float32)
    up_more = jnp.einsum("rlw,lwf->rlf", portion, w_up, preferred_element_type=jnp.float32)
    hidden = (jax.nn.silu(gate_more) * up_more).astype(jnp.bfloat16)
    resplit = lax.all_to_all(w_down, "blk", split_axis=2, concat_axis=1, tiled=True)
    zero_sum = jnp.zeros((slice_width, rows_total * local_count), jnp.float32)
    total = zero_sum
    portion = lax.all_gather(hidden, "blk", axis=2, tiled=True)
    ranges_count = portion.shape[2] // hidden_cut
    for number in range(ranges_count):
        part_hidden = portion[:, :, number * hidden_cut : (number + 1) * hidden_cut]
        part_rows = lax.dynamic_slice_in_dim(resplit, number * hidden_cut, hidden_cut, 1)
        partial_value = jnp.einsum(
            "lfd,rlf->drl", part_rows, part_hidden, preferred_element_type=jnp.float32
        )
        partial_value = partial_value.reshape(slice_width, rows_total * local_count)
        total = total + partial_value.astype(jnp.bfloat16).astype(jnp.float32)
    returned = total.astype(jnp.bfloat16).reshape(
        slice_width, ulysses_size, data_size, capacity, local_count
    )
    returned_rows = lax.all_to_all(
        lax.all_to_all(returned, "uly", split_axis=1, concat_axis=1, tiled=True),
        "dp",
        split_axis=2,
        concat_axis=2,
        tiled=True,
    )
    returned_rows = returned_rows.reshape(slice_width, rows_total * local_count).astype(jnp.float32)
    mixed = lax.dot_general(
        mixing, returned_rows, (((1,), (1,)), ((), ())), precision=lax.Precision.HIGHEST
    )
    return mixed.astype(jnp.bfloat16)


MESH = pl.DeviceIdType.MESH


def neighbours(deep):
    at_y, at_u, at_z = lax.axis_index("blk"), lax.axis_index("uly"), lax.axis_index("dp")
    at_x, core = at_u // 2, at_u % 2
    devices = {
        "up": {"dp": jnp.minimum(at_z + 1, deep - 1)},
        "down": {"dp": jnp.maximum(at_z - 1, 0)},
        "x": {"uly": (1 - at_x) * 2 + core},
        "y": {"blk": 1 - at_y},
        "core": {"uly": at_x * 2 + 1 - core},
    }
    return at_x, at_y, at_z, core, devices


def greet(deep, at_z, devices):
    barrier = pltpu.get_barrier_semaphore()
    for name in ("x", "y", "core"):
        pl.semaphore_signal(barrier, inc=1, device_id=devices[name], device_id_type=MESH)

    @pl.when(at_z > 0)
    def _():
        pl.semaphore_signal(barrier, inc=1, device_id=devices["down"], device_id_type=MESH)

    @pl.when(at_z < deep - 1)
    def _():
        pl.semaphore_signal(barrier, inc=1, device_id=devices["up"], device_id_type=MESH)

    beside = (at_z > 0).astype(jnp.int32) + (at_z < deep - 1).astype(jnp.int32)
    pl.semaphore_wait(barrier, 3 + beside)


def gather_kernel(deep, parts, apart, tok, own_share, every, shares, own_sem, send, recv):
    at_x, at_y, at_z, core, devices = neighbours(deep)
    rows_each, width = tok.shape
    piece = rows_each // parts
    plane = width - apart
    plane_cols = pl.ds(pl.multiple_of(at_y * apart, 128), plane)
    theirs = pl.ds(pl.multiple_of(at_y * plane, 128), apart)
    lacking = pl.ds(pl.multiple_of((1 - at_y) * plane, 128), apart)
    entire = pl.ds(0, width)
    pending = []

    def group(x_of, core_of, z_of):
        return (2 * x_of + core_of) * deep + z_of

    def block(x_of, core_of, z_of, k, cols):
        start = pl.multiple_of(group(x_of, core_of, z_of) * rows_each + k * piece, piece)
        return every.at[pl.ds(start, piece), cols]

    def copy(src, dst, kind, index, to):
        return pltpu.make_async_remote_copy(
            src_ref=src, dst_ref=dst, send_sem=send.at[kind, index], recv_sem=recv.at[kind, index],
            device_id=devices[to], device_id_type=MESH)

    def start(condition, src, dst, kind, index, to):
        def go():
            copy(src, dst, kind, index, to).start()

        if condition is None:
            go()
        else:
            pl.when(condition)(go)
        pending.append((condition, src, dst, kind, index, to))

    def arrive(dst, kind, index):
        copy(dst, dst, kind, index, "x").wait_recv()

    greet(deep, at_z, devices)
    low, high = at_z > 0, at_z < deep - 1
    mine_at = pl.multiple_of(group(at_x, core, at_z) * rows_each, rows_each)
    placed = pltpu.make_async_copy(tok, every.at[pl.ds(mine_at, rows_each)], own_sem.at[0])
    placed.start()
    share_at = shares.at[group(at_x, core, at_z)]
    share_placed = pltpu.make_async_copy(own_share, share_at, own_sem.at[1])
    share_placed.start()
    for k in range(parts):
        here = at_z * parts + k
        source = tok.at[pl.ds(k * piece, piece), plane_cols]
        target = block(at_x, core, at_z, k, plane_cols)
        start(high, source, target, 0, here, "up")
        start(low, source, target, 1, here, "down")
        start(None, source, target, 2, here, "x")
    start(high, own_share, share_at, 9, at_z, "up")
    start(low, own_share, share_at, 10, at_z, "down")
    start(None, own_share, share_at, 11, at_z, "x")
    for k in range(parts):
        start(None, tok.at[pl.ds(k * piece, piece)], block(at_x, core, at_z, k, entire), 5, at_z * parts + k, "core")
    start(None, own_share, share_at, 12, at_z, "core")

    def from_z(condition, onward, kind, to, z_of, k):
        held = block(at_x, core, z_of, k, plane_cols)
        index = z_of * parts + k
        pl.when(condition)(lambda: arrive(held, kind, index))
        start(condition & onward, held, held, kind, index, to)
        start(condition, held, held, 2, index, "x")
        sent = block(at_x, core, z_of, k, theirs)
        start(condition, sent, sent, 3, index, "y")
        start(condition, held, held, 5, index, "core")
        if k == parts - 1:
            share = shares.at[group(at_x, core, z_of)]
            pl.when(condition)(lambda: arrive(share, kind + 9, z_of))
            start(condition & onward, share, share, kind + 9, z_of, to)
            start(condition, share, share, 11, z_of, "x")
            start(condition, share, share, 12, z_of, "core")

    def from_x(condition, z_of, k):
        held = block(1 - at_x, core, z_of, k, plane_cols)
        index = z_of * parts + k
        sent = block(1 - at_x, core, z_of, k, theirs)
        pl.when(condition)(lambda: arrive(held, 2, index))
        start(condition, sent, sent, 4, index, "y")
        start(condition, held, held, 6, index, "core")
        if k == parts - 1:
            share = shares.at[group(1 - at_x, core, z_of)]
            pl.when(condition)(lambda: arrive(share, 11, z_of))
            start(condition, share, share, 13, z_of, "core")

    def below(step):
        return at_z >= step, jnp.maximum(at_z - step, 0)

    def above(step):
        return at_z + step < deep, jnp.minimum(at_z + step, deep - 1)

    def sides(step):
        return [(at_z >= 0, at_z)] if step == 0 else [below(step), above(step)]

    for step in range(1, deep + 1):
        for k in range(parts):
            if step < deep:
                there, z_of = below(step)
                from_z(there, high, 0, "up", z_of, k)
                there, z_of = above(step)
                from_z(there, low, 1, "down", z_of, k)
            for there, z_of in sides(step - 1):
                from_x(there, z_of, k)

    def from_y(condition, x_of, kind, z_of, k):
        held = block(x_of, core, z_of, k, lacking)
        index = z_of * parts + k
        pl.when(condition)(lambda: arrive(held, kind, index))
        start(condition, held, held, kind + 4, index, "core")

    def each_remote(act):
        for step in range(deep):
            for k in range(parts):
                for there, z_of in sides(step):
                    if step > 0:
                        act(there, at_x, 3, z_of, k)
                    act(there, 1 - at_x, 4, z_of, k)

    each_remote(from_y)

    def from_core(condition, x_of, kind, z_of, k):
        index = z_of * parts + k

        @pl.when(condition)
        def _():
            arrive(block(x_of, 1 - core, z_of, k, plane_cols), kind + 2, index)
            arrive(block(x_of, 1 - core, z_of, k, lacking), kind + 4, index)
            if k == parts - 1:
                arrive(shares.at[group(x_of, 1 - core, z_of)], kind + 9, z_of)

    for k in range(parts):
        arrive(block(at_x, 1 - core, at_z, k, entire), 5, at_z * parts + k)
    arrive(shares.at[group(at_x, 1 - core, at_z)], 12, at_z)
    each_remote(from_core)
    placed.wait()
    share_placed.wait()
    for condition, src, dst, kind, index, to in pending:
        def end(src=src, dst=dst, kind=kind, index=index, to=to):
            copy(src, dst, kind, index, to).wait_send()

        if condition is None:
            end()
        else:
            pl.when(condition)(end)


def gather(tokens, share, groups, deep):
    rows_each, width = tokens.shape
    parts = 2
    apart = width * 3 // 8 // 128 * 128
    vmem = pl.BlockSpec(memory_space=pltpu.VMEM)
    return pl.pallas_call(
        lambda *refs: gather_kernel(deep, parts, apart, *refs),
        out_shape=(
            jax.ShapeDtypeStruct((groups * rows_each, width), tokens.dtype),
            jax.ShapeDtypeStruct((groups,) + share.shape, share.dtype),
        ),
        in_specs=[vmem, vmem],
        out_specs=(vmem, vmem),
        scratch_shapes=[
            pltpu.SemaphoreType.DMA((2,)),
            pltpu.SemaphoreType.DMA((14, deep * parts)),
            pltpu.SemaphoreType.DMA((14, deep * parts)),
        ],
        compiler_params=pltpu.CompilerParams(
            collective_id=0, has_side_effects=True, vmem_limit_bytes=40 << 20),
    )(tokens, share)


def scatter_kernel(deep, low_half, high_half, out, total, a1, a2, b1, b2, rising, falling, send, recv):
    at_x, at_y, at_z, core, devices = neighbours(deep)
    rows_each = out.shape[0]
    part = rows_each // 2
    halves = (low_half, high_half)
    pending = []
    order = []
    for number in range((deep + 1) // 2):
        order += [number] if number == deep - 1 - number else [number, deep - 1 - number]

    def copy(src, dst, kind, index, to):
        return pltpu.make_async_remote_copy(
            src_ref=src, dst_ref=dst, send_sem=send.at[kind, index], recv_sem=recv.at[kind, index],
            device_id=devices[to], device_id_type=MESH)

    def start(condition, *what):
        def go():
            copy(*what).start()

        if condition is None:
            go()
        else:
            pl.when(condition)(go)
        pending.append((condition, what))

    def rows_of(x_of, core_of, z_of):
        first = ((2 * x_of + core_of) * deep + z_of) * rows_each
        return pl.ds(pl.multiple_of(first, rows_each), rows_each)

    def added(one, other):
        return (one.astype(jnp.float32) + other.astype(jnp.float32)).astype(jnp.bfloat16)

    greet(deep, at_z, devices)
    for z_of in order:
        for x_of in range(2):
            for half in range(2):
                start(None, halves[half].at[rows_of(x_of, 1 - core, z_of)], total.at[z_of, x_of, half],
                      0, (z_of * 2 + x_of) * 2 + half, "core")
    upper, lower = pl.ds(0, part), pl.ds(part, part)
    for z_of in order:
        for x_of in range(2):
            for half in range(2):
                spot = total.at[z_of, x_of, half]
                copy(spot, spot, 0, (z_of * 2 + x_of) * 2 + half, "core").wait_recv()
                total[z_of, x_of, half] = added(total[z_of, x_of, half], halves[half][rows_of(x_of, core, z_of), :])
        start(None, total.at[z_of, :, 1 - at_y, upper], a1.at[z_of], 1, z_of, "y")
        start(None, total.at[z_of, 1 - at_x, :, lower], b1.at[z_of], 2, z_of, "x")

    def first_stage(z_of):
        copy(a1.at[z_of], a1.at[z_of], 1, z_of, "y").wait_recv()
        for x_of in range(2):
            total[z_of, x_of, at_y, upper] = added(total[z_of, x_of, at_y, upper], a1[z_of, x_of])
        start(None, total.at[z_of, 1 - at_x, at_y, upper], a2.at[z_of], 3, z_of, "x")
        copy(b1.at[z_of], b1.at[z_of], 2, z_of, "x").wait_recv()
        for half in range(2):
            total[z_of, at_x, half, lower] = added(total[z_of, at_x, half, lower], b1[z_of, half])
        start(None, total.at[z_of, at_x, 1 - at_y, lower], b2.at[z_of], 4, z_of, "y")

    def second_stage(z_of):
        copy(a2.at[z_of], a2.at[z_of], 3, z_of, "x").wait_recv()
        total[z_of, at_x, at_y, upper] = added(total[z_of, at_x, at_y, upper], a2[z_of])
        copy(b2.at[z_of], b2.at[z_of], 4, z_of, "y").wait_recv()
        total[z_of, at_x, at_y, lower] = added(total[z_of, at_x, at_y, lower], b2[z_of])

    def third_stage(z_of):
        for toward, farther, inbound, kind, to in (
            (at_z < z_of, at_z > 0, rising, 5, "up"),
            (at_z > z_of, at_z < deep - 1, falling, 6, "down"),
        ):
            @pl.when(toward & farther)
            def _(inbound=inbound, kind=kind, to=to):
                copy(inbound.at[z_of], inbound.at[z_of], kind, z_of, to).wait_recv()
                total[z_of, at_x, at_y] = added(total[z_of, at_x, at_y], inbound[z_of])

            start(toward, total.at[z_of, at_x, at_y], inbound.at[z_of], kind, z_of, to)

    for number in range(deep + 2):
        if number < deep:
            first_stage(order[number])
        if 0 <= number - 1 < deep:
            second_stage(order[number - 1])
        if 0 <= number - 2 < deep:
            third_stage(order[number - 2])

    @pl.when(at_z > 0)
    def _():
        copy(rising.at[at_z], rising.at[at_z], 5, at_z, "up").wait_recv()
        total[at_z, at_x, at_y] = added(total[at_z, at_x, at_y], rising[at_z])

    @pl.when(at_z < deep - 1)
    def _():
        copy(falling.at[at_z], falling.at[at_z], 6, at_z, "down").wait_recv()
        total[at_z, at_x, at_y] = added(total[at_z, at_x, at_y], falling[at_z])

    out[...] = total[at_z, at_x, at_y]
    for condition, what in pending:
        def end(what=what):
            copy(*what).wait_send()

        if condition is None:
            end()
        else:
            pl.when(condition)(end)


def scatter(low_half, high_half, rows_each, deep):
    width = low_half.shape[1]
    part = rows_each // 2
    kind = low_half.dtype
    vmem = pl.BlockSpec(memory_space=pltpu.VMEM)
    return pl.pallas_call(
        lambda *refs: scatter_kernel(deep, *refs),
        out_shape=jax.ShapeDtypeStruct((rows_each, width), kind),
        in_specs=[vmem, vmem],
        out_specs=vmem,
        scratch_shapes=[
            pltpu.VMEM((deep, 2, 2, rows_each, width), kind),
            pltpu.VMEM((deep, 2, part, width), kind),
            pltpu.VMEM((deep, part, width), kind),
            pltpu.VMEM((deep, 2, part, width), kind),
            pltpu.VMEM((deep, part, width), kind),
            pltpu.VMEM((deep, rows_each, width), kind),
            pltpu.VMEM((deep, rows_each, width), kind),
            pltpu.SemaphoreType.DMA((7, deep * 4)),
            pltpu.SemaphoreType.DMA((7, deep * 4)),
        ],
        compiler_params=pltpu.CompilerParams(
            collective_id=1, has_side_effects=True, vmem_limit_bytes=48 << 20),
    )(low_half, high_half)


def local_dense(tokens, expert_ids, route_weight, w_gate, w_up, w_down):
    deep = lax.axis_size("dp")
    groups = lax.axis_size("uly") * deep
    rows_each = tokens.shape[0]
    labels = lax.broadcasted_iota(jnp.int32, (groups, 1, 1), 0)
    scaled = jnp.sum(jnp.where(expert_ids[None] == labels, route_weight[None], 0.0), axis=2)
    scaled = jnp.pad(scaled, ((0, 0), (0, -rows_each % 128)))
    everyone, shares = gather(tokens, scaled, groups, deep)
    first = lax.axis_index("uly") * deep + lax.axis_index("dp")
    share = lax.dynamic_slice_in_dim(shares, first, 1, 1)[:, 0, :rows_each].reshape(groups * rows_each, 1)
    gate = jnp.dot(everyone, w_gate[0], preferred_element_type=jnp.float32)
    up = jnp.dot(everyone, w_up[0], preferred_element_type=jnp.float32)
    hidden = (jax.nn.silu(gate) * up * share).astype(jnp.bfloat16)
    half = w_down.shape[2] // 2
    low_half = jnp.dot(hidden, w_down[0, :, :half], preferred_element_type=jnp.float32).astype(jnp.bfloat16)
    high_half = jnp.dot(hidden, w_down[0, :, half:], preferred_element_type=jnp.float32).astype(jnp.bfloat16)
    return scatter(low_half, high_half, rows_each, deep)


def solution(mesh):
    groups = mesh.shape["uly"] * mesh.shape["dp"]
    dense = mesh.shape["blk"] == 2 and mesh.shape["uly"] == 4 and groups <= 16
    return jax.shard_map(
        local_dense if dense else local_slots,
        mesh=mesh,
        in_specs=(
            P(("uly", "dp"), None),
            P(("uly", "dp"), None),
            P(("uly", "dp"), None),
            P(("uly", "dp"), None, "blk"),
            P(("uly", "dp"), None, "blk"),
            P(("uly", "dp"), "blk", None),
        ),
        out_specs=P(("uly", "dp"), "blk"),
        check_vma=False,
    )
```

profile of v0, /device:TPU:18, one launch (start us, length us, event | category | flops | bytes accessed | tf_op | source)
XLA Modules:
  0.0 131.7 jit_solution(12932249947474507887)
XLA Ops:
  0.0 0.7 select_reduce_fusion
  0.7 0.0 copy-start
  0.8 1.0 copy-done
  1.8 39.8 %shard_map.64 = (bf16[1024,4096]{1,0:T(8,128)(2,1)S(1)}, f32[16,16,128]{2,1,0:T(8,128)S(1)}) custom-call(bf16[64,4096]{1,0:T(8,128)(2,1)S(1)} %copy-done, f32[16,128]{1,0:T(8,128)S(1)} %pad.4.refs_1_), custom_call_target="tpu_custom_call" | custom-call | tf_op jit(solution)/shard_map/pallas_call | solution.py:272
  41.6 0.0 copy-start.1
  41.6 3.2 %copy-done.1 = bf16[1024,4096]{1,0:T(8,128)(2,1)} copy-done((bf16[1024,4096]{1,0:T(8,128)(2,1)}, bf16[1024,4096]{1,0:T(8,128)(2,1)S(1)}, u32[]{:S(2)}) %copy-start.1) | copy-done | bytes 8388632
  44.8 0.1 mul.23
  44.9 0.0 copy-start.2
  44.9 0.0 copy-start.3
  44.9 8.3 %fusion.2 = f32[1024,512]{1,0:T(8,128)S(1)} fusion(bf16[1024,4096]{1,0:T(8,128)(2,1)} %copy-done.1, bf16[1,4096,512]{2,1,0:T(8,128)(2,1)} %param.9), kind=kOutput, calls=%fused_computation.2 | convolution fusion | flops 4294967296 | bytes 14680064 | tf_op jit(solution)/shard_map/dot_general | solution.py:431
  53.2 0.0 copy-done.2
  53.2 0.0 copy-done.3
  53.2 0.0 copy-start.4
  53.2 4.8 %multiply_convert_fusion = bf16[1024,512]{1,0:T(8,128)(2,1)S(1)} fusion(f32[1024,512]{1,0:T(8,128)S(1)} %fusion.2, bf16[1024,4096]{1,0:T(8,128)(2,1)S(1)} %copy-done.2, bf16[1,4096,512]{2,1,0:T(8,128)(2,1)S(1)} %copy-done.3, f32[1024]{0:T(1024)S(1)} %mul.23), kind=kOutput, calls=%fused_computation.10 | convolution fusion | flops 4298637312 | bytes 15732736 | tf_op jit(solution)/shard_map/dot_general | solution.py:432
  58.0 0.0 copy-done.4
  58.0 4.3 %convolution_convert_fusion.refs_1_ = bf16[1024,2048]{1,0:T(8,128)(2,1)} fusion(bf16[1024,512]{1,0:T(8,128)(2,1)S(1)} %multiply_convert_fusion, bf16[1,512,4096]{2,1,0:T(8,128)(2,1)S(1)} %copy-done.4), kind=kOutput, calls=%fused_computation.4 | convolution fusion | flops 2149580800 | bytes 7340032 | tf_op jit(solution)/shard_map/dot_general | solution.py:436
  62.3 2.3 %convolution_convert_fusion.1.refs_0_ = bf16[1024,2048]{1,0:T(8,128)(2,1)S(1)} fusion(bf16[1024,512]{1,0:T(8,128)(2,1)S(1)} %multiply_convert_fusion, bf16[1,512,4096]{2,1,0:T(8,128)(2,1)S(1)} %copy-done.4), kind=kOutput, calls=%fused_computation.5 | convolution fusion | flops 2149580800 | bytes 7340032 | tf_op jit(solution)/shard_map/dot_general | solution.py:435
  64.6 66.4 %shard_map.65 = bf16[64,2048]{1,0:T(8,128)(2,1)S(1)} custom-call(bf16[1024,2048]{1,0:T(8,128)(2,1)S(1)} %convolution_convert_fusion.1.refs_0_, bf16[1024,2048]{1,0:T(8,128)(2,1)} %convolution_convert_fusion.refs_1_), custom_call_target="tpu_custom_call" | custom-call | tf_op jit(solution)/shard_map/pallas_call | solution.py:400
  131.0 0.7 copy.10
  (2 shorter events, 0.0 us)
Async XLA Ops:
  0.7 1.0 copy-start
  41.6 3.2 %copy-start.1 = (bf16[1024,4096]{1,0:T(8,128)(2,1)}, bf16[1024,4096]{1,0:T(8,128)(2,1)S(1)}, u32[]{:S(2)}) copy-start(bf16[1024,4096]{1,0:T(8,128)(2,1)S(1)} %get-tuple-element.7) | copy-start | bytes 25165828
  44.9 8.3 %copy-start.2 = (bf16[1024,4096]{1,0:T(8,128)(2,1)S(1)}, bf16[1024,4096]{1,0:T(8,128)(2,1)}, u32[]{:S(2)}) copy-start(bf16[1024,4096]{1,0:T(8,128)(2,1)} %copy-done.1) | copy-start | bytes 25165828
  44.9 8.3 %copy-start.3 = (bf16[1,4096,512]{2,1,0:T(8,128)(2,1)S(1)}, bf16[1,4096,512]{2,1,0:T(8,128)(2,1)}, u32[]{:S(2)}) copy-start(bf16[1,4096,512]{2,1,0:T(8,128)(2,1)} %param.10) | copy-start | bytes 12582916
  53.2 4.8 %copy-start.4 = (bf16[1,512,4096]{2,1,0:T(8,128)(2,1)S(1)}, bf16[1,512,4096]{2,1,0:T(8,128)(2,1)}, u32[]{:S(2)}) copy-start(bf16[1,512,4096]{2,1,0:T(8,128)(2,1)} %param.11) | copy-start | bytes 12582916
where the time goes:
time: 132 us
  Pallas kernels  106 us (80%)
  matrix products  19.6 us (15%)
  local copies, waits for them, and re-layouts  5.07 us (4%)
    pallas_call x1, Pallas kernels, scatter(): pl.pallas_call(lambda *refs: scatter_kernel(deep, *refs), out_shape=jax.S...  66.4 us
    pallas_call x1, Pallas kernels, gather(): pl.pallas_call(lambda *refs: gather_kernel(deep, parts, apart, *refs), ou...  39.8 us
    dot_general x1, matrix products, local_dense(): gate = jnp.dot(everyone, w_gate[0], preferred_element_type=jnp.float32)  8.27 us
    unnamed x11, local copies, waits for them, and re-layouts  4.97 us
    dot_general x1, matrix products, local_dense(): up = jnp.dot(everyone, w_up[0], preferred_element_type=jnp.float32)  4.75 us
    dot_general x1, matrix products, local_dense(): jnp.dot(hidden, w_down[0, :, half:], preferred_element_type=jnp.float32)  4.28 us

commit v1 on v0

v1 whole, which is shorter than its diff:
```python
import jax
import jax.numpy as jnp
from jax import lax
from jax.experimental import pallas as pl
from jax.experimental.pallas import tpu as pltpu
from jax.sharding import PartitionSpec as P


def routing_tables(expert_ids, route_weight, groups, local_count, capacity):
    tokens_here, picks_count = expert_ids.shape
    experts = groups * local_count
    labels = lax.broadcasted_iota(jnp.int32, (1, 1, experts), 2)
    onehot = (expert_ids[:, :, None] == labels).astype(jnp.int32)
    chosen = jnp.sum(onehot, axis=1)
    before = jnp.cumsum(chosen, axis=0) - chosen
    slot_of = jnp.sum(onehot * before[:, None, :], axis=2)
    places = lax.broadcasted_iota(jnp.int32, (1, 1, capacity), 2)
    slot_hot = (slot_of[:, :, None] == places).astype(jnp.float32)
    expert_hot = onehot.astype(jnp.float32).reshape(tokens_here, picks_count, groups, local_count)
    placing = jnp.einsum("tkgl,tkc->gclt", expert_hot, slot_hot)
    placing = placing.reshape(groups * capacity * local_count, tokens_here)
    mixing = jnp.einsum("tkgl,tkc,tk->tgcl", expert_hot, slot_hot, route_weight)
    mixing = mixing.reshape(tokens_here, groups * capacity * local_count)
    return (placing.astype(jnp.bfloat16), mixing)


def local_slots(tokens, expert_ids, route_weight, w_gate, w_up, w_down):
    ulysses_size = lax.axis_size("uly")
    data_size = lax.axis_size("dp")
    cycle_size = lax.axis_size("blk")
    tokens_here, model_width = tokens.shape
    local_count = w_gate.shape[0]
    hidden_cut = w_gate.shape[2]
    groups = ulysses_size * data_size
    experts = groups * local_count
    picks_count = expert_ids.shape[1]
    capacity = min(tokens_here, max(2, 5 * tokens_here * picks_count // (4 * experts)))
    placing, mixing = routing_tables(expert_ids, route_weight, groups, local_count, capacity)
    slice_width = model_width // cycle_size
    rows_total = groups * capacity
    cycle_index = lax.axis_index("blk")
    own_part = lax.dynamic_slice_in_dim(tokens, cycle_index * slice_width, slice_width, 1)
    outgoing = jnp.dot(placing, own_part, preferred_element_type=jnp.float32).astype(jnp.bfloat16)
    outgoing = outgoing.reshape(ulysses_size, data_size, capacity, local_count, slice_width)
    arrived = lax.all_to_all(
        lax.all_to_all(outgoing, "uly", split_axis=0, concat_axis=0, tiled=True),
        "dp",
        split_axis=1,
        concat_axis=1,
        tiled=True,
    )
    arrived = arrived.reshape(rows_total, local_count, slice_width)
    portion = lax.all_gather(arrived, "blk", axis=2, tiled=True)
    gate_more = jnp.einsum("rlw,lwf->rlf", portion, w_gate, preferred_element_type=jnp.float32)
    up_more = jnp.einsum("rlw,lwf->rlf", portion, w_up, preferred_element_type=jnp.float32)
    hidden = (jax.nn.silu(gate_more) * up_more).astype(jnp.bfloat16)
    resplit = lax.all_to_all(w_down, "blk", split_axis=2, concat_axis=1, tiled=True)
    zero_sum = jnp.zeros((slice_width, rows_total * local_count), jnp.float32)
    total = zero_sum
    portion = lax.all_gather(hidden, "blk", axis=2, tiled=True)
    ranges_count = portion.shape[2] // hidden_cut
    for number in range(ranges_count):
        part_hidden = portion[:, :, number * hidden_cut : (number + 1) * hidden_cut]
        part_rows = lax.dynamic_slice_in_dim(resplit, number * hidden_cut, hidden_cut, 1)
        partial_value = jnp.einsum(
            "lfd,rlf->drl", part_rows, part_hidden, preferred_element_type=jnp.float32
        )
        partial_value = partial_value.reshape(slice_width, rows_total * local_count)
        total = total + partial_value.astype(jnp.bfloat16).astype(jnp.float32)
    returned = total.astype(jnp.bfloat16).reshape(
        slice_width, ulysses_size, data_size, capacity, local_count
    )
    returned_rows = lax.all_to_all(
        lax.all_to_all(returned, "uly", split_axis=1, concat_axis=1, tiled=True),
        "dp",
        split_axis=2,
        concat_axis=2,
        tiled=True,
    )
    returned_rows = returned_rows.reshape(slice_width, rows_total * local_count).astype(jnp.float32)
    mixed = lax.dot_general(
        mixing, returned_rows, (((1,), (1,)), ((), ())), precision=lax.Precision.HIGHEST
    )
    return mixed.astype(jnp.bfloat16)


MESH = pl.DeviceIdType.MESH

PLANE, BY_Z, PARTS, SUB = 21 * 128, 0 * 128, 2, 1


def schedule():
    steps = []

    def add(*words):
        for word in words:
            when = word[0] if word[0] in "ei" else ""
            word = word[len(when):]
            steps.append((when, word, word[0], [int(digit) for digit in word[1:]]))

    add("Z10", "iZ20", "X00", "Z11", "iZ21", "X01", "Y100", "eZ20", "iZ30", "X10", "iY200", "Y010")
    add("iZ31", "iX20", "Y101", "eZ21", "iY201", "X11", "Y011", "C0", "G00", "eZ30", "eX20", "eY200")
    add("iX21", "iY300", "G01", "Y110", "D00", "D01", "eY201", "eZ31", "eX21", "iX30", "iY301", "iY210")
    add("iX31", "Y111", "iM00", "iM01", "iY211", "C1", "G10", "eX30", "eY300", "G11", "eY210", "iY310")
    add("D10", "D11", "eX31", "eY301", "eM00", "eM01", "eY211", "iY311", "C2", "G20", "eY310", "iF020")
    add("G21", "eY311", "iF000", "ia0", "D20", "iF030", "D21", "eF020", "C3", "G30", "eF000", "iF010")
    add("M20", "G31", "eF030", "M21", "D30", "eF010", "D31", "ib00", "ib10", "M30", "M31", "F200")
    add("F220", "eA20", "iM10", "iM11", "F210", "F230", "eM10", "eM11", "F300", "iF320", "iF310", "iF330")
    add("S300", "eF320", "eS320", "eF310", "eS310", "eF330", "eS330", "eB200", "eS210", "eB210", "eS230", "F100")
    add("F120", "A10", "iS320", "F110", "F130", "iS310", "iS200", "iS330", "B100", "iB110", "iS220", "S110")
    add("eB110", "iS210", "S130", "eL00", "eL20", "ea0", "iS230", "L10", "L30", "eb00", "eb10")
    return steps


SCHEDULE = schedule()


def neighbours(deep):
    at_y, at_u, at_z = lax.axis_index("blk"), lax.axis_index("uly"), lax.axis_index("dp")
    at_x, core = at_u // 2, at_u % 2
    devices = {
        "up": {"dp": jnp.minimum(at_z + 1, deep - 1)},
        "down": {"dp": jnp.maximum(at_z - 1, 0)},
        "x": {"uly": (1 - at_x) * 2 + core},
        "y": {"blk": 1 - at_y},
        "core": {"uly": at_x * 2 + 1 - core},
    }
    return at_x, at_y, at_z, core, devices


def greet_all(deep, at_z, devices):
    barrier = pltpu.get_barrier_semaphore()
    for name in ("x", "y", "core"):
        pl.semaphore_signal(barrier, inc=1, device_id=devices[name], device_id_type=MESH)

    @pl.when(at_z > 0)
    def _():
        pl.semaphore_signal(barrier, inc=1, device_id=devices["down"], device_id_type=MESH)

    @pl.when(at_z < deep - 1)
    def _():
        pl.semaphore_signal(barrier, inc=1, device_id=devices["up"], device_id_type=MESH)


def greet_wait(deep, at_z):
    barrier = pltpu.get_barrier_semaphore()
    beside = (at_z > 0).astype(jnp.int32) + (at_z < deep - 1).astype(jnp.int32)
    pl.semaphore_wait(barrier, 3 + beside)


def orders(deep):
    return [sorted(range(deep), key=lambda p: (abs(p - z), (p < z) == (2 * z < deep))) for z in range(deep)]


def fused_kernel(deep, plane, by_z, parts, tok, ids_hbm, weight_hbm, gate_hbm, up_hbm, down_hbm, out,
                 every, w_gate, w_up, w_down, ids, weight, hidden, part, total, ya, xb, zin, fin, own_sem, send, recv):
    at_x, at_y, at_z, core, devices = neighbours(deep)
    rows_each, width = tok.shape
    wide = every.shape[1]
    half_width = width // 2
    piece = rows_each // parts
    slab = rows_each // 2
    slice_rows = slab // SUB
    apart = wide - plane
    low, high = at_z > 0, at_z < deep - 1
    ends = (at_z == 0) | (at_z == deep - 1)
    inner = (at_z > 0) & (at_z < deep - 1)
    first_cols = at_y * apart
    plane_cols = pl.ds(pl.multiple_of(first_cols, 128), plane)
    theirs = pl.ds(pl.multiple_of(at_y * plane, 128), apart)
    lacking = pl.ds(pl.multiple_of((1 - at_y) * plane, 128), apart)
    x_cols = pl.ds(pl.multiple_of(first_cols + at_y * by_z, 128), plane - by_z)
    z_cols = pl.ds(pl.multiple_of(first_cols + (1 - at_y) * (plane - by_z), 128), max(by_z, 128))
    entire = pl.ds(0, wide)
    arrivals = orders(deep)

    def table(rows, k):
        return sum((at_z == z).astype(jnp.int32) * rows[z][k] for z in range(deep))

    planes = [at_z] + [table(arrivals, k) for k in range(1, deep)]
    pending = []
    only = [None]

    def device(to):
        return devices[to] if isinstance(to, str) else to

    def copy(src, dst, kind, index, to):
        return pltpu.make_async_remote_copy(
            src_ref=src, dst_ref=dst, send_sem=send.at[kind, index], recv_sem=recv.at[kind, index],
            device_id=device(to), device_id_type=MESH)

    def start(condition, *what):
        def go():
            copy(*what).start()

        if only[0] is not None:
            condition = only[0] if condition is None else only[0] & condition
        if condition is None:
            go()
        else:
            pl.when(condition)(go)
        pending.append((condition, what))

    def do(go):
        if only[0] is None:
            go()
        else:
            pl.when(only[0])(go)

    def given(condition, act):
        before = only[0]
        only[0] = condition if before is None else before & condition
        act()
        only[0] = before

    def arrive(dst, kind, index):
        do(lambda: copy(dst, dst, kind, index, "x").wait_recv())

    def block(x_of, core_of, z_of, p, cols):
        first = (z_of * 4 + 2 * x_of + core_of) * rows_each + p * piece
        return every.at[pl.ds(pl.multiple_of(first, piece), piece), cols]

    def from_below(z_of):
        return z_of < at_z

    def toward(step):
        return {"dp": jnp.clip(at_z + step, 0, deep - 1)}

    def within(z_of):
        return (z_of >= 0) & (z_of < deep)

    def z_arrives(k, p):
        z_of = planes[k]
        index = z_of * parts + p
        step = jnp.where(from_below(z_of), 1, -1)
        kind = jnp.where(from_below(z_of), 0, 1)
        held = block(at_x, core, z_of, p, plane_cols)
        arrive(held, kind, index)
        start(within(at_z + step), held, held, kind, index, toward(step))
        along = block(at_x, core, z_of, p, x_cols)
        start(None, along, along, 4, index, "x")
        sent = block(at_x, core, z_of, p, theirs)
        start(None, sent, sent, 5, index, "y")
        start(None, held, held, 7, index, "core")

    def x_arrives(k, p):
        z_of = planes[k]
        index = z_of * parts + p
        held = block(1 - at_x, core, z_of, p, plane_cols if k == 0 else x_cols)
        arrive(held, 4, index)
        sent = block(1 - at_x, core, z_of, p, theirs)
        start(None, sent, sent, 6, index, "y")
        if k == 0 and by_z:
            extra = block(1 - at_x, core, z_of, p, z_cols)
            start(high, extra, extra, 2, index, "up")
            start(low, extra, extra, 3, index, "down")
        start(None, held, held, 9, index, "core")

    def h_arrives(k, p):
        z_of = planes[k]
        index = z_of * parts + p
        step = jnp.where(from_below(z_of), 1, -1)
        kind = jnp.where(from_below(z_of), 2, 3)
        held = block(1 - at_x, core, z_of, p, z_cols)
        arrive(held, kind, index)
        start(within(at_z + step), held, held, kind, index, toward(step))
        start(None, held, held, 10, index, "core")

    def y_arrives(k, other, p):
        z_of = planes[k]
        index = z_of * parts + p
        held = block(1 - at_x if other else at_x, core, z_of, p, lacking)
        arrive(held, 6 if other else 5, index)
        start(None, held, held, 11 if other else 8, index, "core")

    def complete(k):
        z_of = planes[k]
        for p in range(parts):
            index = z_of * parts + p
            arrive(block(at_x, 1 - core, z_of, p, entire if k == 0 else plane_cols), 7, index)
            if k > 0:
                arrive(block(at_x, 1 - core, z_of, p, lacking), 8, index)
                if by_z:
                    arrive(block(1 - at_x, 1 - core, z_of, p, z_cols), 10, index)
            arrive(block(1 - at_x, 1 - core, z_of, p, plane_cols if k == 0 else x_cols), 9, index)
            arrive(block(1 - at_x, 1 - core, z_of, p, lacking), 11, index)

    batch = 4 * rows_each
    expert = (2 * at_x + core) * deep + at_z
    experts = 4 * deep

    def gate_up(k, n):
        span = w_gate.shape[1] // 2
        rows = pl.ds(pl.multiple_of(planes[k] * batch, batch), batch)
        cols = pl.ds(n * span, span)
        features = every[rows, 0:width]
        gate = jnp.dot(features, w_gate[:, cols], preferred_element_type=jnp.float32)
        up = jnp.dot(features, w_up[:, cols], preferred_element_type=jnp.float32)
        shares = every[rows, width:wide].astype(jnp.float32)
        lane = lax.broadcasted_iota(jnp.int32, shares.shape, 1)
        mine = (lane == expert) | (lane == expert + experts)
        share = jnp.sum(jnp.where(mine, shares, 0.0), axis=1, keepdims=True)
        hidden[:, cols] = (jax.nn.silu(gate) * up * share).astype(jnp.bfloat16)

    def down(k, n):
        half = (1 - at_y) if n == 0 else at_y
        span = half_width // 2
        z_of = planes[k]

        @pl.loop(0, 2)
        def _(m):
            cols = pl.ds(pl.multiple_of(half * half_width + m * span, span), span)
            value = jnp.dot(hidden[...], w_down[:, cols], preferred_element_type=jnp.float32).astype(jnp.bfloat16)
            into = pl.ds(pl.multiple_of(m * span, span), span)
            for g in range(4):
                part[z_of, g, half, :, into] = value[g * rows_each:(g + 1) * rows_each]

        for x_of in range(2):
            start(None, part.at[z_of, 2 * x_of + 1 - core, half], total.at[z_of, x_of, half],
                  12, (z_of * 2 + x_of) * 2 + half, "core")

    upper, lower = pl.ds(0, slab), pl.ds(slab, slab)

    def added(one, other):
        return (one.astype(jnp.float32) + other.astype(jnp.float32)).astype(jnp.bfloat16)

    def strip(base, s):
        return pl.ds(base + s * slice_rows, slice_rows)

    def halves_meet(k, n):
        half = (1 - at_y) if n == 0 else at_y
        z_of = planes[k]
        for x_of in (1 - at_x, at_x):
            spot = total.at[z_of, x_of, half]
            arrive(spot, 12, (z_of * 2 + x_of) * 2 + half)
            add_to(spot, part.at[z_of, 2 * x_of + core, half])
            for s in range(SUB):
                if n == 0:
                    start(None, total.at[z_of, x_of, half, strip(0, s)], ya.at[z_of, x_of, strip(0, s)],
                          13, (z_of * 2 + x_of) * SUB + s, "y")
                if x_of is not at_x:
                    start(None, total.at[z_of, x_of, half, strip(slab, s)], xb.at[z_of, half, strip(0, s)],
                          14, (z_of * 2 + half) * SUB + s, "x")

    def quarter(z_of, q, s):
        if q < 2:
            return total.at[z_of, (1 - at_x) if q == 0 else at_x, at_y, strip(0, s)]
        return total.at[z_of, at_x, (1 - at_y) if q == 2 else at_y, strip(slab, s)]

    def add_to(spot, other):
        def go():
            spot[...] = added(spot[...], other[...])

        do(go)

    def first_sum(k, q, s):
        z_of = planes[k]
        if q < 2:
            x_of = (1 - at_x) if q == 0 else at_x
            came, kind, index = ya.at[z_of, x_of, strip(0, s)], 13, z_of * 2 + x_of
        else:
            half = (1 - at_y) if q == 2 else at_y
            came, kind, index = xb.at[z_of, half, strip(0, s)], 14, z_of * 2 + half
        arrive(came, kind, index * SUB + s)
        add_to(quarter(z_of, q, s), came)

    def second_send(k, s):
        z_of = planes[k]
        for n, to in ((0, "x"), (1, "y")):
            start(None, quarter(z_of, 2 * n, s), fin.at[z_of, n, strip(0, s)], 17 + n, z_of * SUB + s, to)

    def second_sum(k, n, s):
        z_of = planes[k]
        came = fin.at[z_of, n, strip(0, s)]
        arrive(came, 17 + n, z_of * SUB + s)
        add_to(quarter(z_of, 2 * n + 1, s), came)

    def z_stage(k, q, s):
        z_of = planes[k]
        rises = z_of > at_z
        step = jnp.where(rises, 1, -1)
        side = jnp.where(rises, 0, 1)
        index = (z_of * 4 + q) * SUB + s
        spot = quarter(z_of, q, s)
        came = zin.at[side, z_of, q, strip(0, s)]

        def inbound():
            arrive(came, 15 + side, index)
            add_to(spot, came)

        given(within(at_z - step), inbound)
        start(None, spot, came, 15 + side, index, toward(step))

    def z_last(q, s):
        for side, condition in ((0, low), (1, high)):
            def inbound(side=side):
                came = zin.at[side, at_z, q, strip(0, s)]
                arrive(came, 15 + side, (at_z * 4 + q) * SUB + s)
                add_to(quarter(at_z, q, s), came)

            given(condition, inbound)

    mine = pl.ds(pl.multiple_of((at_z * 4 + 2 * at_x + core) * rows_each, rows_each), rows_each)
    placed = pltpu.make_async_copy(tok, every.at[mine, pl.ds(0, width)], own_sem.at[0])
    placed.start()
    weights = [pltpu.make_async_copy(src, dst, own_sem.at[1 + n])
               for n, (src, dst) in enumerate(((gate_hbm, w_gate), (up_hbm, w_up), (down_hbm, w_down)))]
    for each in weights:
        each.start()
    picks = [pltpu.make_async_copy(src, dst, own_sem.at[4 + n])
             for n, (src, dst) in enumerate(((ids_hbm, ids), (weight_hbm, weight)))]
    for each in picks:
        each.start()
    greet_all(deep, at_z, devices)
    for each in picks:
        each.wait()
    shape = (wide - width, rows_each)
    lane = lax.broadcasted_iota(jnp.int32, shape, 0)
    named = jnp.where(lane < experts, lane, lane - experts)
    scaled = jnp.zeros(shape, jnp.float32)
    for pick in range(ids.shape[0]):
        scaled = scaled + jnp.where(ids[pick:pick + 1, :] == named, weight[pick:pick + 1, :], 0.0)
    rough = scaled.astype(jnp.bfloat16).astype(jnp.float32)
    every[mine, width:wide] = jnp.where(lane < experts, rough, scaled - rough).T.astype(jnp.bfloat16)
    with jax.named_scope("greet"):
        greet_wait(deep, at_z)
    with jax.named_scope("placed"):
        placed.wait()
    for p in range(parts):
        index = at_z * parts + p
        held = block(at_x, core, at_z, p, plane_cols)
        start(high, held, held, 0, index, "up")
        start(low, held, held, 1, index, "down")
        start(None, held, held, 4, index, "x")
    for p in range(parts):
        whole = block(at_x, core, at_z, p, entire)
        start(None, whole, whole, 7, at_z * parts + p, "core")

    acts = {
        "Z": z_arrives, "X": x_arrives, "H": h_arrives, "Y": y_arrives, "C": complete,
        "G": gate_up, "D": down, "M": halves_meet,
        "F": first_sum, "A": second_send, "B": second_sum, "S": z_stage, "L": z_last,
        "a": lambda s: second_send(0, s),
        "b": lambda n, s: second_sum(0, n, s),
    }
    waited = [False]
    for when, word, name, numbers in SCHEDULE:
        if name == "G" and not waited[0]:
            waited[0] = True
            with jax.named_scope("weights"):
                for each in weights:
                    each.wait()
        only[0] = {"": None, "e": ends, "i": inner}[when]
        with jax.named_scope(word):
            acts[name](*numbers)
    only[0] = None
    out[...] = total[at_z, at_x, at_y]
    with jax.named_scope("drain"):
        for condition, what in pending:
            def end(what=what):
                copy(*what).wait_send()

            if condition is None:
                end()
            else:
                pl.when(condition)(end)


def local_dense(tokens, expert_ids, route_weight, w_gate, w_up, w_down):
    deep = lax.axis_size("dp")
    rows_each, width = tokens.shape
    hidden_cut = w_gate.shape[2]
    half = width // 2
    wide = width + 128
    plane = PLANE
    by_z = BY_Z
    parts = PARTS
    slab = rows_each // 2
    kind = tokens.dtype
    vmem = pl.BlockSpec(memory_space=pltpu.VMEM)
    hbm = pl.BlockSpec(memory_space=pl.ANY)
    return pl.pallas_call(
        lambda *refs: fused_kernel(deep, plane, by_z, parts, *refs),
        out_shape=jax.ShapeDtypeStruct((rows_each, half), kind),
        in_specs=[hbm] * 6,
        out_specs=vmem,
        scratch_shapes=[
            pltpu.VMEM((deep * 4 * rows_each, wide), kind),
            pltpu.VMEM((width, hidden_cut), kind),
            pltpu.VMEM((width, hidden_cut), kind),
            pltpu.VMEM((hidden_cut, width), kind),
            pltpu.VMEM(expert_ids.shape[::-1], expert_ids.dtype),
            pltpu.VMEM(route_weight.shape[::-1], route_weight.dtype),
            pltpu.VMEM((4 * rows_each, hidden_cut), kind),
            pltpu.VMEM((deep, 4, 2, rows_each, half), kind),
            pltpu.VMEM((deep, 2, 2, rows_each, half), kind),
            pltpu.VMEM((deep, 2, slab, half), kind),
            pltpu.VMEM((deep, 2, slab, half), kind),
            pltpu.VMEM((2, deep, 4, slab, half), kind),
            pltpu.VMEM((deep, 2, slab, half), kind),
            pltpu.SemaphoreType.DMA((6,)),
            pltpu.SemaphoreType.DMA((19, deep * 4 * max(SUB, PARTS // 2))),
            pltpu.SemaphoreType.DMA((19, deep * 4 * max(SUB, PARTS // 2))),
        ],
        compiler_params=pltpu.CompilerParams(
            collective_id=0, has_side_effects=True, vmem_limit_bytes=60 << 20),
    )(tokens, expert_ids.T, route_weight.T, w_gate[0], w_up[0], w_down[0])


def solution(mesh):
    dense = mesh.shape["blk"] == 2 and mesh.shape["uly"] == 4 and mesh.shape["dp"] == 4
    return jax.shard_map(
        local_dense if dense else local_slots,
        mesh=mesh,
        in_specs=(
            P(("uly", "dp"), None),
            P(("uly", "dp"), None),
            P(("uly", "dp"), None),
            P(("uly", "dp"), None, "blk"),
            P(("uly", "dp"), None, "blk"),
            P(("uly", "dp"), "blk", None),
        ),
        out_specs=P(("uly", "dp"), "blk"),
        check_vma=False,
    )
```

time: 132 us -> 92.3 us (0.70)
  the two profiles are of different devices: /device:TPU:18 before, /device:TPU:0 now
where the time goes in v1:
time: 92.3 us; the launch traced here: 92.2 us
  Pallas kernels  90.5 us (98%)
  local copies, waits for them, and re-layouts  1.67 us (2%)
    pallas_call x1, Pallas kernels, local_dense(): pl.pallas_call(lambda *refs: fused_kernel(deep, plane, by_z, parts, *refs...  90.5 us

profile of v1, /device:TPU:0, one launch (start us, length us, event | category | flops | bytes accessed | tf_op | source)
XLA Modules:
  0.0 92.2 jit_solution(8842546952866349437)
XLA Ops:
  0.0 90.5 %shard_map.64 = bf16[64,2048]{1,0:T(8,128)(2,1)} custom-call(bf16[64,4096]{1,0:T(8,128)(2,1)} %refs_0_.1, s32[8,64]{1,0:T(8,128)} %bitcast.8, f32[8,64]{1,0:T(8,128)} %bitcast.9, bf16[4096,512]{1,0:T(8,128)(2,1)} %bitcast.5, bf16[4096,512]{1,0:T(8,128)(2,1)} %bitcast.6, bf16[512,4096]{1,0:T(8,128)(2,1)} %bitcast.7), custom_call_target="tpu_custom_call" | custom-call | tf_op jit(solution)/shard_map/pallas_call | solution.py:482
  90.5 1.7 %copy.8 = bf16[64,2048]{1,0:T(8,128)(2,1)} copy(bf16[64,2048]{1,0:T(8,128)(2,1)} %shard_map.64) | data formatting | bytes 524288

commit v2 on v1

--- a/solution.py
+++ b/solution.py
@@ -86,33 +86,33 @@
 
 MESH = pl.DeviceIdType.MESH
 
-PLANE, BY_Z, PARTS, SUB = 21 * 128, 0 * 128, 2, 1
-
-
-def schedule():
-    steps = []
-
-    def add(*words):
-        for word in words:
-            when = word[0] if word[0] in "ei" else ""
-            word = word[len(when):]
-            steps.append((when, word, word[0], [int(digit) for digit in word[1:]]))
-
-    add("Z10", "iZ20", "X00", "Z11", "iZ21", "X01", "Y100", "eZ20", "iZ30", "X10", "iY200", "Y010")
-    add("iZ31", "iX20", "Y101", "eZ21", "iY201", "X11", "Y011", "C0", "G00", "eZ30", "eX20", "eY200")
-    add("iX21", "iY300", "G01", "Y110", "D00", "D01", "eY201", "eZ31", "eX21", "iX30", "iY301", "iY210")
-    add("iX31", "Y111", "iM00", "iM01", "iY211", "C1", "G10", "eX30", "eY300", "G11", "eY210", "iY310")
-    add("D10", "D11", "eX31", "eY301", "eM00", "eM01", "eY211", "iY311", "C2", "G20", "eY310", "iF020")
-    add("G21", "eY311", "iF000", "ia0", "D20", "iF030", "D21", "eF020", "C3", "G30", "eF000", "iF010")
-    add("M20", "G31", "eF030", "M21", "D30", "eF010", "D31", "ib00", "ib10", "M30", "M31", "F200")
-    add("F220", "eA20", "iM10", "iM11", "F210", "F230", "eM10", "eM11", "F300", "iF320", "iF310", "iF330")
-    add("S300", "eF320", "eS320", "eF310", "eS310", "eF330", "eS330", "eB200", "eS210", "eB210", "eS230", "F100")
-    add("F120", "A10", "iS320", "F110", "F130", "iS310", "iS200", "iS330", "B100", "iB110", "iS220", "S110")
-    add("eB110", "iS210", "S130", "eL00", "eL20", "ea0", "iS230", "L10", "L30", "eb00", "eb10")
-    return steps
-
-
-SCHEDULE = schedule()
+PLANE, BY_Z, PARTS, SUB = 22 * 128, 2 * 128, 4, 2
+VMEM_LIMIT = 67043328 - (288 << 10)
+
+
+SCHEDULE = (
+    100, 200200, 1000, 110, 200210, 1010, 120, 200220, 1020, 3100, 203200, 200130,
+    200230, 202200, 202210, 201030, 3010, 100130, 101030, 3101, 202220, 201100, 200300, 203201,
+    202100, 3011, 101100, 100200, 202230, 201200, 3102, 102100, 200310, 202110, 203202, 201110,
+    3012, 101110, 200320, 202120, 3103, 100210, 102110, 201210, 203203, 200330, 202300, 202310,
+    202130, 202320, 201120, 202330, 3013, 101120, 3110, 100220, 102120, 201220, 203300, 4000,
+    5000, 203210, 1130, 103200, 103111, 100230, 5010, 102130, 101200, 103201, 103112, 203301,
+    203111, 6000, 100300, 102200, 101210, 103202, 201230, 203302, 6010, 103113, 101220, 100310,
+    102210, 103203, 103210, 101230, 100320, 102220, 103300, 1300, 3211, 100330, 102300, 203303,
+    201310, 203112, 3212, 102310, 102230, 102320, 102330, 101310, 103301, 201320, 203113, 3213,
+    101320, 103302, 201330, 3310, 101330, 103303, 3311, 3312, 3313, 4300, 5300, 7000,
+    7010, 5310, 6300, 6310, 4200, 5200, 8000, 8020, 213000, 7300, 5210, 8001,
+    8021, 213100, 7310, 6200, 8010, 8030, 6210, 8011, 8031, 4100, 5100, 108300,
+    110300, 108320, 110320, 214000, 214100, 7200, 5110, 108301, 110301, 108321, 110321, 208300,
+    208320, 7210, 108310, 110310, 108330, 110330, 6100, 208301, 208321, 6110, 208310, 214010,
+    210300, 8311, 110311, 208330, 207100, 210320, 207110, 8331, 110331, 214110, 210301, 8200,
+    8220, 109200, 107100, 210321, 210200, 8201, 8221, 109210, 107110, 210310, 210220, 8210,
+    8230, 210330, 210201, 8211, 8231, 111200, 110210, 111210, 110230, 210311, 210221, 8100,
+    8120, 9100, 112000, 210331, 210210, 8101, 8121, 9110, 112200, 113000, 111201, 210230,
+    208110, 208130, 10211, 108110, 112010, 8111, 108130, 112210, 113100, 111211, 208131, 10231,
+    108131, 112100, 11100, 10110, 11110, 10130, 112300, 11101, 10111, 11111, 10131, 212100,
+    212300, 12110, 114000, 114100, 12310, 114010, 114110,
+)
 
 
 def neighbours(deep):
@@ -146,6 +146,15 @@
     barrier = pltpu.get_barrier_semaphore()
     beside = (at_z > 0).astype(jnp.int32) + (at_z < deep - 1).astype(jnp.int32)
     pl.semaphore_wait(barrier, 3 + beside)
+
+
+def semaphore_slots(deep):
+    pieces, extra = deep * PARTS, deep * PARTS if BY_Z else 0
+    return (
+        ("z", pieces), ("h", extra), ("x", pieces), ("ys", pieces), ("yo", pieces), ("c", deep), ("m", deep * 2),
+        ("fy", deep * 2 * SUB), ("fx", deep * 2 * SUB), ("s", deep * 4 * SUB), ("t", 4 * SUB),
+        ("bx", deep * SUB), ("by", deep * SUB),
+    )
 
 
 def orders(deep):
@@ -184,12 +193,21 @@
     def device(to):
         return devices[to] if isinstance(to, str) else to
 
-    def copy(src, dst, kind, index, to):
+    slots, count = {}, 0
+    for name, size in semaphore_slots(deep):
+        slots[name] = count
+        count += size
+    names = ("z", "h", "x", "x0", "ys", "yo", "cz", "cz0", "cx", "cx0", "ch", "cys", "cyo", "m", "fy", "fx", "s", "s0", "bx", "by")
+    sends = {name: number for number, name in enumerate(names)}
+
+    def copy(src, dst, send_at, recv_at, to):
         return pltpu.make_async_remote_copy(
-            src_ref=src, dst_ref=dst, send_sem=send.at[kind, index], recv_sem=recv.at[kind, index],
+            src_ref=src, dst_ref=dst, send_sem=send.at[send_at], recv_sem=recv.at[recv_at],
             device_id=device(to), device_id_type=MESH)
 
-    def start(condition, *what):
+    def start(condition, src, dst, kind, index, to, other=None):
+        what = (src, dst, other if other is not None and not isinstance(other, str) else sends[other or kind], slots[kind] + index, to)
+
         def go():
             copy(*what).start()
 
@@ -214,7 +232,30 @@
         only[0] = before
 
     def arrive(dst, kind, index):
-        do(lambda: copy(dst, dst, kind, index, "x").wait_recv())
+        at = slots[kind] + index
+        do(lambda: copy(dst, dst, at, at, "x").wait_recv())
+
+    def group_rows(x_of, core_of, z_of, cols):
+        first = (z_of * 4 + 2 * x_of + core_of) * rows_each
+        return every.at[pl.ds(pl.multiple_of(first, rows_each), rows_each), cols]
+
+    seen, doubled, stages = {}, set(), {}
+
+    def pass_on(key, held, kind, z_of):
+        done = {}
+        for kind_of in (1, 2):
+            if word_for[0] in (0, kind_of):
+                seen[key, kind_of] = seen.get((key, kind_of), 0) + 1
+                done[kind_of] = seen[key, kind_of] == parts
+        whole = [name for name in done if done[name]]
+        if not whole:
+            return
+        if len(whole) == len(done):
+            start(None, held, held, "c", z_of, "core", kind)
+        else:
+            given(ends if whole[0] == 1 else inner, lambda: start(None, held, held, "c", z_of, "core", kind))
+
+    word_for = [0]
 
     def block(x_of, core_of, z_of, p, cols):
         first = (z_of * 4 + 2 * x_of + core_of) * rows_each + p * piece
@@ -233,57 +274,47 @@
         z_of = planes[k]
         index = z_of * parts + p
         step = jnp.where(from_below(z_of), 1, -1)
-        kind = jnp.where(from_below(z_of), 0, 1)
         held = block(at_x, core, z_of, p, plane_cols)
-        arrive(held, kind, index)
-        start(within(at_z + step), held, held, kind, index, toward(step))
+        arrive(held, "z", index)
+        start(within(at_z + step), held, held, "z", index, toward(step))
         along = block(at_x, core, z_of, p, x_cols)
-        start(None, along, along, 4, index, "x")
+        start(None, along, along, "x", index, "x")
         sent = block(at_x, core, z_of, p, theirs)
-        start(None, sent, sent, 5, index, "y")
-        start(None, held, held, 7, index, "core")
+        start(None, sent, sent, "ys", index, "y")
+        pass_on(("z", k), group_rows(at_x, core, z_of, plane_cols), "cz", z_of)
 
     def x_arrives(k, p):
         z_of = planes[k]
         index = z_of * parts + p
-        held = block(1 - at_x, core, z_of, p, plane_cols if k == 0 else x_cols)
-        arrive(held, 4, index)
+        cols = plane_cols if k == 0 else x_cols
+        held = block(1 - at_x, core, z_of, p, cols)
+        arrive(held, "x", index)
         sent = block(1 - at_x, core, z_of, p, theirs)
-        start(None, sent, sent, 6, index, "y")
+        start(None, sent, sent, "yo", index, "y")
         if k == 0 and by_z:
             extra = block(1 - at_x, core, z_of, p, z_cols)
-            start(high, extra, extra, 2, index, "up")
-            start(low, extra, extra, 3, index, "down")
-        start(None, held, held, 9, index, "core")
+            start(high, extra, extra, "h", index, "up")
+            start(low, extra, extra, "h", index, "down")
+        pass_on(("x", k), group_rows(1 - at_x, core, z_of, cols), "cx" if k else "cx0", z_of)
 
     def h_arrives(k, p):
         z_of = planes[k]
         index = z_of * parts + p
         step = jnp.where(from_below(z_of), 1, -1)
-        kind = jnp.where(from_below(z_of), 2, 3)
         held = block(1 - at_x, core, z_of, p, z_cols)
-        arrive(held, kind, index)
-        start(within(at_z + step), held, held, kind, index, toward(step))
-        start(None, held, held, 10, index, "core")
+        arrive(held, "h", index)
+        start(within(at_z + step), held, held, "h", index, toward(step))
+        pass_on(("h", k), group_rows(1 - at_x, core, z_of, z_cols), "ch", z_of)
 
     def y_arrives(k, other, p):
         z_of = planes[k]
         index = z_of * parts + p
-        held = block(1 - at_x if other else at_x, core, z_of, p, lacking)
-        arrive(held, 6 if other else 5, index)
-        start(None, held, held, 11 if other else 8, index, "core")
+        x_of = 1 - at_x if other else at_x
+        arrive(block(x_of, core, z_of, p, lacking), "yo" if other else "ys", index)
+        pass_on(("y", k, other), group_rows(x_of, core, z_of, lacking), "cyo" if other else "cys", z_of)
 
     def complete(k):
-        z_of = planes[k]
-        for p in range(parts):
-            index = z_of * parts + p
-            arrive(block(at_x, 1 - core, z_of, p, entire if k == 0 else plane_cols), 7, index)
-            if k > 0:
-                arrive(block(at_x, 1 - core, z_of, p, lacking), 8, index)
-                if by_z:
-                    arrive(block(1 - at_x, 1 - core, z_of, p, z_cols), 10, index)
-            arrive(block(1 - at_x, 1 - core, z_of, p, plane_cols if k == 0 else x_cols), 9, index)
-            arrive(block(1 - at_x, 1 - core, z_of, p, lacking), 11, index)
+        arrive(every.at[pl.ds(0, 2 * rows_each), :], "c", planes[k])
 
     batch = 4 * rows_each
     expert = (2 * at_x + core) * deep + at_z
@@ -317,7 +348,7 @@
 
         for x_of in range(2):
             start(None, part.at[z_of, 2 * x_of + 1 - core, half], total.at[z_of, x_of, half],
-                  12, (z_of * 2 + x_of) * 2 + half, "core")
+                  "m", z_of * 2 + half, "core")
 
     upper, lower = pl.ds(0, slab), pl.ds(slab, slab)
 
@@ -330,17 +361,17 @@
     def halves_meet(k, n):
         half = (1 - at_y) if n == 0 else at_y
         z_of = planes[k]
+        arrive(total.at[z_of, :, half], "m", z_of * 2 + half)
         for x_of in (1 - at_x, at_x):
             spot = total.at[z_of, x_of, half]
-            arrive(spot, 12, (z_of * 2 + x_of) * 2 + half)
             add_to(spot, part.at[z_of, 2 * x_of + core, half])
             for s in range(SUB):
                 if n == 0:
                     start(None, total.at[z_of, x_of, half, strip(0, s)], ya.at[z_of, x_of, strip(0, s)],
-                          13, (z_of * 2 + x_of) * SUB + s, "y")
+                          "fy", (z_of * 2 + x_of) * SUB + s, "y")
                 if x_of is not at_x:
                     start(None, total.at[z_of, x_of, half, strip(slab, s)], xb.at[z_of, half, strip(0, s)],
-                          14, (z_of * 2 + half) * SUB + s, "x")
+                          "fx", (z_of * 2 + half) * SUB + s, "x")
 
     def quarter(z_of, q, s):
         if q < 2:
@@ -357,22 +388,22 @@
         z_of = planes[k]
         if q < 2:
             x_of = (1 - at_x) if q == 0 else at_x
-            came, kind, index = ya.at[z_of, x_of, strip(0, s)], 13, z_of * 2 + x_of
+            came, kind, index = ya.at[z_of, x_of, strip(0, s)], "fy", z_of * 2 + x_of
         else:
             half = (1 - at_y) if q == 2 else at_y
-            came, kind, index = xb.at[z_of, half, strip(0, s)], 14, z_of * 2 + half
+            came, kind, index = xb.at[z_of, half, strip(0, s)], "fx", z_of * 2 + half
         arrive(came, kind, index * SUB + s)
         add_to(quarter(z_of, q, s), came)
 
     def second_send(k, s):
         z_of = planes[k]
         for n, to in ((0, "x"), (1, "y")):
-            start(None, quarter(z_of, 2 * n, s), fin.at[z_of, n, strip(0, s)], 17 + n, z_of * SUB + s, to)
+            start(None, quarter(z_of, 2 * n, s), fin.at[z_of, n, strip(0, s)], "b" + to, z_of * SUB + s, to)
 
     def second_sum(k, n, s):
         z_of = planes[k]
         came = fin.at[z_of, n, strip(0, s)]
-        arrive(came, 17 + n, z_of * SUB + s)
+        arrive(came, "by" if n else "bx", z_of * SUB + s)
         add_to(quarter(z_of, 2 * n + 1, s), came)
 
     def z_stage(k, q, s):
@@ -385,17 +416,20 @@
         came = zin.at[side, z_of, q, strip(0, s)]
 
         def inbound():
-            arrive(came, 15 + side, index)
+            arrive(came, "s", index)
             add_to(spot, came)
 
         given(within(at_z - step), inbound)
-        start(None, spot, came, 15 + side, index, toward(step))
+        names = ["s0" if (kind_of, k) in doubled else "s" for kind_of in (word_for[0] or 1, word_for[0] or 2)]
+        chosen = names[0] if names[0] == names[1] else jnp.where(ends, sends[names[0]], sends[names[1]])
+        landing = jnp.where((at_z + step == z_of) & (step < 0), slots["t"] - slots["s"] + q * SUB + s, index)
+        start(None, spot, came, "s", landing, toward(step), chosen)
 
     def z_last(q, s):
         for side, condition in ((0, low), (1, high)):
             def inbound(side=side):
                 came = zin.at[side, at_z, q, strip(0, s)]
-                arrive(came, 15 + side, (at_z * 4 + q) * SUB + s)
+                arrive(came, "t" if side else "s", q * SUB + s + (0 if side else at_z * 4 * SUB))
                 add_to(quarter(at_z, q, s), came)
 
             given(condition, inbound)
@@ -405,15 +439,14 @@
     placed.start()
     weights = [pltpu.make_async_copy(src, dst, own_sem.at[1 + n])
                for n, (src, dst) in enumerate(((gate_hbm, w_gate), (up_hbm, w_up), (down_hbm, w_down)))]
-    for each in weights:
-        each.start()
     picks = [pltpu.make_async_copy(src, dst, own_sem.at[4 + n])
              for n, (src, dst) in enumerate(((ids_hbm, ids), (weight_hbm, weight)))]
     for each in picks:
         each.start()
     greet_all(deep, at_z, devices)
-    for each in picks:
-        each.wait()
+    with jax.named_scope("picks"):
+        for each in picks:
+            each.wait()
     shape = (wide - width, rows_each)
     lane = lax.broadcasted_iota(jnp.int32, shape, 0)
     named = jnp.where(lane < experts, lane, lane - experts)
@@ -426,44 +459,76 @@
         greet_wait(deep, at_z)
     with jax.named_scope("placed"):
         placed.wait()
+    for each in weights:
+        each.start()
     for p in range(parts):
         index = at_z * parts + p
         held = block(at_x, core, at_z, p, plane_cols)
-        start(high, held, held, 0, index, "up")
-        start(low, held, held, 1, index, "down")
-        start(None, held, held, 4, index, "x")
-    for p in range(parts):
-        whole = block(at_x, core, at_z, p, entire)
-        start(None, whole, whole, 7, at_z * parts + p, "core")
-
-    acts = {
-        "Z": z_arrives, "X": x_arrives, "H": h_arrives, "Y": y_arrives, "C": complete,
-        "G": gate_up, "D": down, "M": halves_meet,
-        "F": first_sum, "A": second_send, "B": second_sum, "S": z_stage, "L": z_last,
-        "a": lambda s: second_send(0, s),
-        "b": lambda n, s: second_sum(0, n, s),
-    }
+        start(high, held, held, "z", index, "up")
+        start(low, held, held, "z", index, "down")
+        start(None, held, held, "x", index, "x", "x0")
+    whole = group_rows(at_x, core, at_z, entire)
+    start(None, whole, whole, "c", at_z, "core", "cz0")
+
+    acts = (
+        (z_arrives, 2), (x_arrives, 2), (h_arrives, 2), (y_arrives, 3), (complete, 1), (gate_up, 2), (down, 2),
+        (halves_meet, 2), (first_sum, 3), (second_send, 2), (z_stage, 3), (second_sum, 3), (z_last, 2),
+        (lambda s: second_send(0, s), 1), (lambda n, s: second_sum(0, n, s), 2),
+    )
     waited = [False]
-    for when, word, name, numbers in SCHEDULE:
-        if name == "G" and not waited[0]:
+    for kind_of in (1, 2):
+        found = {(step // 100 % 10, step // 10 % 10) for step in SCHEDULE
+                 if step // 1000 % 100 == 10 and step // 100000 in (0, kind_of)}
+        both = {k for k, q in found if q == 0}
+        stages[kind_of] = (len(both), len({k for k, q in found} - both))
+        doubled.update((kind_of, k) for k in both)
+    for step in SCHEDULE:
+        when, (act, taken) = step // 100000, acts[step // 1000 % 100]
+        numbers = (step // 100 % 10, step // 10 % 10, step % 10)[:taken]
+        if act is gate_up and not waited[0]:
             waited[0] = True
             with jax.named_scope("weights"):
                 for each in weights:
                     each.wait()
-        only[0] = {"": None, "e": ends, "i": inner}[when]
-        with jax.named_scope(word):
-            acts[name](*numbers)
+        only[0] = (None, ends, inner)[when]
+        word_for[0] = when
+        with jax.named_scope(str(step)):
+            act(*numbers)
     only[0] = None
     out[...] = total[at_z, at_x, at_y]
+    def drain(name, ref):
+        at = sends[name]
+        pltpu.make_async_remote_copy(
+            src_ref=ref, dst_ref=ref, send_sem=send.at[at], recv_sem=recv.at[0],
+            device_id=devices["x"], device_id_type=MESH).wait_send()
+
+    def some(groups, cols):
+        return every.at[pl.ds(0, groups * rows_each), cols]
+
     with jax.named_scope("drain"):
-        for condition, what in pending:
-            def end(what=what):
-                copy(*what).wait_send()
-
-            if condition is None:
-                end()
-            else:
-                pl.when(condition)(end)
+        for name, groups, cols in (
+            ("x0", 1, plane_cols), ("x", deep - 1, x_cols), ("ys", deep - 1, theirs), ("yo", deep, theirs),
+            ("cz0", 1, entire), ("cz", deep - 1, plane_cols), ("cx0", 1, plane_cols), ("cx", deep - 1, x_cols),
+            ("cys", deep - 1, lacking), ("cyo", deep, lacking),
+        ):
+            drain(name, some(groups, cols))
+        if by_z:
+            drain("ch", some(deep - 1, z_cols))
+        for name, ref in (("m", total), ("fy", ya), ("fx", xb)):
+            drain(name, ref)
+        for kind_of, condition in ((1, ends), (2, inner)):
+            @pl.when(condition)
+            def _(kind_of=kind_of):
+                drain("z", some(1 if kind_of == 1 else deep + 1, plane_cols))
+                if by_z:
+                    drain("h", some(1 if kind_of == 1 else deep + 1, z_cols))
+                both, one = stages[kind_of]
+                if both:
+                    drain("s0", zin.at[0, pl.ds(0, both)])
+                if one:
+                    drain("s", zin.at[1, pl.ds(0, one), pl.ds(0, 2)])
+                for name, n in (("bx", 0), ("by", 1)):
+                    drain(name, fin.at[pl.ds(0, one + 1), n])
 
 
 def local_dense(tokens, expert_ids, route_weight, w_gate, w_up, w_down):
@@ -499,11 +564,11 @@
             pltpu.VMEM((2, deep, 4, slab, half), kind),
             pltpu.VMEM((deep, 2, slab, half), kind),
             pltpu.SemaphoreType.DMA((6,)),
-            pltpu.SemaphoreType.DMA((19, deep * 4 * max(SUB, PARTS // 2))),
-            pltpu.SemaphoreType.DMA((19, deep * 4 * max(SUB, PARTS // 2))),
+            pltpu.SemaphoreType.DMA((20,)),
+            pltpu.SemaphoreType.DMA((sum(size for _, size in semaphore_slots(deep)),)),
         ],
         compiler_params=pltpu.CompilerParams(
-            collective_id=0, has_side_effects=True, vmem_limit_bytes=60 << 20),
+            collective_id=0, has_side_effects=True, vmem_limit_bytes=VMEM_LIMIT),
     )(tokens, expert_ids.T, route_weight.T, w_gate[0], w_up[0], w_down[0])
 
 

time: 92.3 us -> 78.9 us (0.85)
  Pallas kernels: 90.5 us -> 77.1 us
    pallas_call x1, Pallas kernels: 90.5 us -> 77.1 us  [local_dense(): pl.pallas_call(lambda *refs: fused_kernel(deep, plane, by_z, parts, *refs...]
where the time goes in v2:
time: 78.9 us; the launch traced here: 78.8 us
  Pallas kernels  77.1 us (98%)
  local copies, waits for them, and re-layouts  1.67 us (2%)
    pallas_call x1, Pallas kernels, local_dense(): pl.pallas_call(lambda *refs: fused_kernel(deep, plane, by_z, parts, *refs...  77.1 us
    unnamed x1, local copies, waits for them, and re-layouts  1.67 us

profile of v2, /device:TPU:0, one launch (start us, length us, event | category | flops | bytes accessed | tf_op | source)
XLA Modules:
  0.0 78.8 jit_solution(3471692954318960869)
XLA Ops:
  0.0 77.1 %shard_map.64 = bf16[64,2048]{1,0:T(8,128)(2,1)} custom-call(bf16[64,4096]{1,0:T(8,128)(2,1)} %refs_0_.1, s32[8,64]{1,0:T(8,128)} %bitcast.8, f32[8,64]{1,0:T(8,128)} %bitcast.9, bf16[4096,512]{1,0:T(8,128)(2,1)} %bitcast.5, bf16[4096,512]{1,0:T(8,128)(2,1)} %bitcast.6, bf16[512,4096]{1,0:T(8,128)(2,1)} %bitcast.7), custom_call_target="tpu_custom_call" | custom-call | tf_op jit(solution)/shard_map/pallas_call | solution.py:547
  77.1 1.7 %copy.8 = bf16[64,2048]{1,0:T(8,128)(2,1)} copy(bf16[64,2048]{1,0:T(8,128)(2,1)} %shard_map.64) | data formatting | bytes 524288

commit v3 on v2

--- a/solution.py
+++ b/solution.py
@@ -86,32 +86,30 @@
 
 MESH = pl.DeviceIdType.MESH
 
-PLANE, BY_Z, PARTS, SUB = 22 * 128, 2 * 128, 4, 2
-VMEM_LIMIT = 67043328 - (288 << 10)
+PLANE, BY_Z, PARTS, SUB = 22 * 128, 2 * 128, 4, 1
+VMEM_LIMIT = 54700 << 10
 
 
 SCHEDULE = (
-    100, 200200, 1000, 110, 200210, 1010, 120, 200220, 1020, 3100, 203200, 200130,
-    200230, 202200, 202210, 201030, 3010, 100130, 101030, 3101, 202220, 201100, 200300, 203201,
-    202100, 3011, 101100, 100200, 202230, 201200, 3102, 102100, 200310, 202110, 203202, 201110,
-    3012, 101110, 200320, 202120, 3103, 100210, 102110, 201210, 203203, 200330, 202300, 202310,
-    202130, 202320, 201120, 202330, 3013, 101120, 3110, 100220, 102120, 201220, 203300, 4000,
-    5000, 203210, 1130, 103200, 103111, 100230, 5010, 102130, 101200, 103201, 103112, 203301,
-    203111, 6000, 100300, 102200, 101210, 103202, 201230, 203302, 6010, 103113, 101220, 100310,
-    102210, 103203, 103210, 101230, 100320, 102220, 103300, 1300, 3211, 100330, 102300, 203303,
-    201310, 203112, 3212, 102310, 102230, 102320, 102330, 101310, 103301, 201320, 203113, 3213,
-    101320, 103302, 201330, 3310, 101330, 103303, 3311, 3312, 3313, 4300, 5300, 7000,
-    7010, 5310, 6300, 6310, 4200, 5200, 8000, 8020, 213000, 7300, 5210, 8001,
-    8021, 213100, 7310, 6200, 8010, 8030, 6210, 8011, 8031, 4100, 5100, 108300,
-    110300, 108320, 110320, 214000, 214100, 7200, 5110, 108301, 110301, 108321, 110321, 208300,
-    208320, 7210, 108310, 110310, 108330, 110330, 6100, 208301, 208321, 6110, 208310, 214010,
-    210300, 8311, 110311, 208330, 207100, 210320, 207110, 8331, 110331, 214110, 210301, 8200,
-    8220, 109200, 107100, 210321, 210200, 8201, 8221, 109210, 107110, 210310, 210220, 8210,
-    8230, 210330, 210201, 8211, 8231, 111200, 110210, 111210, 110230, 210311, 210221, 8100,
-    8120, 9100, 112000, 210331, 210210, 8101, 8121, 9110, 112200, 113000, 111201, 210230,
-    208110, 208130, 10211, 108110, 112010, 8111, 108130, 112210, 113100, 111211, 208131, 10231,
-    108131, 112100, 11100, 10110, 11110, 10130, 112300, 11101, 10111, 11111, 10131, 212100,
-    212300, 12110, 114000, 114100, 12310, 114010, 114110,
+    200100, 200200, 1000, 100100, 200110, 200210, 201020, 201030, 1010, 101020, 200220, 203101,
+    120, 101030, 200130, 200230, 200310, 200300, 202230, 3011, 103012, 100110, 101100, 202200,
+    200320, 201220, 202210, 200330, 203103, 3010, 100130, 3102, 1120, 201110, 203012, 201210,
+    3013, 100200, 202220, 2100, 100210, 203201, 203300, 203202, 202330, 202310, 203200, 203203,
+    201130, 203301, 201100, 203112, 202130, 202300, 4000, 5000, 102130, 103103, 101110, 103100,
+    100220, 201230, 5010, 101130, 203212, 6000, 103112, 203113, 202110, 201310, 2120, 103200,
+    100230, 103111, 101210, 203110, 202320, 201300, 201200, 6010, 100310, 102110, 103101, 103113,
+    101220, 100300, 101200, 103203, 103110, 103201, 100320, 203311, 203213, 203111, 203100, 203210,
+    203211, 203303, 201330, 201320, 207000, 4100, 5100, 101230, 100330, 103202, 101310, 207010,
+    203310, 5110, 103210, 203302, 203313, 203312, 6100, 101320, 101300, 103302, 6110, 102300,
+    102200, 102210, 102220, 102320, 103300, 103212, 101330, 103213, 102310, 102330, 7100, 103311,
+    103303, 103310, 102230, 103211, 103301, 107110, 103312, 103313, 4300, 5300, 5310, 108100,
+    108120, 109100, 6300, 207110, 6310, 207300, 4200, 5200, 107300, 5210, 108110, 111100,
+    110110, 107310, 6200, 108300, 110300, 107200, 207310, 6210, 208000, 207200, 208300, 8320,
+    210300, 208120, 10320, 207210, 208030, 208130, 208200, 210200, 8310, 107210, 108200, 208100,
+    208110, 208330, 210310, 209100, 8220, 110310, 108330, 108130, 109200, 210220, 10330, 107000,
+    8210, 108230, 111110, 111200, 110210, 107010, 111210, 108000, 110230, 112000, 8020, 8010,
+    211100, 211110, 210210, 210110, 213000, 208230, 210230, 10130, 108030, 112200, 113000, 212100,
+    14000, 112100, 214100, 12300, 114100,
 )
 
 

time: 78.9 us -> 77.6 us (0.984)
  Pallas kernels: 77.1 us -> 75.3 us
    pallas_call x1, Pallas kernels: 77.1 us -> 75.3 us  [local_dense(): pl.pallas_call(lambda *refs: fused_kernel(deep, plane, by_z, parts, *refs...]
    unnamed x1 -> x5, local copies, waits for them, and re-layouts: 1.67 us -> 2.08 us
where the time goes in v3:
time: 77.6 us; the launch traced here: 77.4 us
  Pallas kernels  75.3 us (97%)
  local copies, waits for them, and re-layouts  2.08 us (3%)
    pallas_call x1, Pallas kernels, local_dense(): pl.pallas_call(lambda *refs: fused_kernel(deep, plane, by_z, parts, *refs...  75.3 us
    unnamed x5, local copies, waits for them, and re-layouts  2.08 us

profile of v3, /device:TPU:0, one launch (start us, length us, event | category | flops | bytes accessed | tf_op | source)
XLA Modules:
  0.0 77.4 jit_solution(10278871426148113008)
XLA Ops:
  0.0 0.0 copy-start
  0.0 0.7 copy-done
  0.7 0.0 copy-start.1
  0.7 0.7 copy-done.1
  1.4 75.3 %shard_map.64 = bf16[64,2048]{1,0:T(8,128)(2,1)S(1)} custom-call(bf16[64,4096]{1,0:T(8,128)(2,1)} %refs_0_.1, s32[8,64]{1,0:T(8,128)S(1)} %bitcast.5, f32[8,64]{1,0:T(8,128)S(1)} %bitcast.6, bf16[4096,512]{1,0:T(8,128)(2,1)} %bitcast.7, bf16[4096,512]{1,0:T(8,128)(2,1)} %bitcast.8, bf16[512,4096]{1,0:T(8,128)(2,1)} %bitcast.9), custom_call_target="tpu_custom_call" | custom-call | tf_op jit(solution)/shard_map/pallas_call | solution.py:545
  76.7 0.7 copy.8
Async XLA Ops:
  0.0 0.7 copy-start
  0.7 0.7 copy-start.1
